TPU v7x, 128 devices: a whole 4x4x4 slice. The times are simulated.
128 devices in a mesh: layer: 8 (over y_hi, x), width: 16 (over y_lo, z, core).
Axes of the slice: x: 4, y: 4 (y_hi: 2, y_lo: 2; y = y_hi * 2 + y_lo), z: 4, core: 2. Of those that a mesh axis runs over, the one named last changes fastest.
Arguments:
- source: bfloat16 [8, 4096, 4096], P('layer', 'width'), may hold values from -6 to 6
- expand_out: bfloat16 [2560, 4096], P(None, 'width'), may hold values from -0.125 to 0.125
- expand_in: bfloat16 [2560, 4096], P(('layer', 'width')), may hold values from -0.09375 to 0.09375
- depth: float32 [16, 8], P('layer'), may hold values from -1.4 to 1.4
Outputs:
- grown: float32 [16, 2560, 2560], P('layer', 'width')
All inputs are finite; a program needn't handle non-finite values.
Results may differ from a plain program's by a relative error of at most 0.018.
Values may be sent and summed in bfloat16 or wider, within the bound.
A program may use at most 128 MiB of HBM per device.

v0:
```python
import jax
import jax.numpy as jnp
from jax import lax
from jax.sharding import Mesh
from jax.sharding import PartitionSpec as P

LAYER_WIDTH = ("layer_0", "layer_1", "width")
LAYER = ("layer_0", "layer_1")


def in_order(parts, dim):
    parts = jnp.moveaxis(parts, 0, dim)
    dims = parts.shape
    return parts.reshape(*dims[:dim], dims[dim] * dims[dim + 1], *dims[dim + 2 :])


def stacked_from(value, axes, order):
    parts = value[None]
    for k in order:
        parts = lax.all_gather(parts, axes[k], axis=0, tiled=True)
    current = [lax.axis_size(axes[k]) for k in reversed(order)]
    parts = parts.reshape(*current, *value.shape)
    turned = sorted(range(len(order)), key=lambda place: order[len(order) - 1 - place])
    return parts.transpose(*turned, *range(len(order), parts.ndim)).reshape(-1, *value.shape)


def gathered_by_axis(value, axes, order, dim):
    return in_order(stacked_from(value, axes, order), dim)


def on_device(source, expand_out, expand_in, depth):
    src_held, row_count, inner_width = source.shape
    stacked = source.reshape(src_held * row_count, inner_width)
    projected = lax.dot_general(
        stacked,
        lax.all_gather(expand_in, LAYER_WIDTH, axis=0, tiled=True),
        (((1,), (1,)), ((), ())),
        preferred_element_type=jnp.float32,
    )
    columns = projected.shape[1]
    projected = projected.astype(jnp.bfloat16).reshape(src_held, row_count, columns)
    own_rows = expand_out.shape[0] // lax.axis_size("width")
    partial_value = jnp.einsum(
        "ri,kic->rkc", expand_out, projected, preferred_element_type=jnp.float32
    ).astype(jnp.bfloat16)
    partial_value = lax.optimization_barrier(partial_value)
    summed = lax.psum_scatter(
        partial_value.astype(jnp.float32)
        .reshape(own_rows * lax.axis_size("width"), src_held * columns)
        .astype(jnp.bfloat16),
        "width",
        scatter_dimension=0,
        tiled=True,
    )
    expanded = summed.reshape(own_rows, src_held, columns)
    return jnp.einsum(
        "tm,rmc->trc",
        depth,
        gathered_by_axis(expanded, LAYER, (0, 1), 1).astype(jnp.float32),
        precision=lax.Precision.HIGHEST,
        preferred_element_type=jnp.float32,
    )


def solution(mesh):
    finer = Mesh(mesh.devices.reshape(2, 4, mesh.shape["width"]), ("layer_0", "layer_1", "width"))
    return jax.shard_map(
        on_device,
        mesh=finer,
        in_specs=(P(LAYER, "width", None), P(None, "width"), P(LAYER_WIDTH, None), P(LAYER, None)),
        out_specs=P(LAYER, "width", None),
        check_vma=False,
    )
```

profile of v0, /device:TPU:1, one launch (start us, length us, event | category | flops | bytes accessed | tf_op | source)
XLA Modules:
  0.0 518.2 jit_solution(15276849728186745125)
XLA Ops:
  6.5 0.0 copy-start
  6.5 0.0 all-gather.10.cloned.1.call-start
  6.5 0.7 all-gather.10.cloned.1.call-update
  7.3 0.0 copy-start.3
  7.3 0.0 reduce-scatter.4.cloned.1.call-start
  7.3 228.3 %all-gather.10.cloned.1.call-done = bf16[128,20,4096]{2,1,0:T(8,128)(2,1)} async-done(((bf16[1,20,4096]{2,1,0:T(8,128)(2,1)}), bf16[128,20,4096]{2,1,0:T(8,128)(2,1)}) %all-gather.10.cloned.1.call-update) | async-done | bytes 20971536 | tf_op jit(solution)/shard_map/all_gather | solution.py:36
  235.6 26.5 %reshape.25 = bf16[2560,4096]{1,0:T(8,128)(2,1)} reshape(bf16[128,20,4096]{2,1,0:T(8,128)(2,1)} %all-gather.10.cloned.1.call-done) | data formatting | bytes 41943040
  262.1 0.0 copy-done
  262.1 0.0 copy-done.3
  262.1 16.7 %fusion = bf16[2560,1,2560]{0,2,1:T(8,128)(2,1)} fusion(bf16[2560,256]{1,0:T(8,128)(2,1)S(1)} %copy-done.3, bf16[2560,4096]{1,0:T(8,128)(2,1)} %reshape.25, bf16[1,256,4096]{2,1,0:T(8,128)(2,1)S(1)} %copy-done), kind=kOutput, calls=%fused_computation.1 | convolution fusion | flops 8731361280 | bytes 37486592 | tf_op jit(solution)/shard_map/ri,kic->rkc/dot_general | solution.py:43
  278.8 17.6 %copy.14 = bf16[2560,2560]{1,0:T(8,128)(2,1)} copy(bf16[2560,2560]{0,1:T(8,128)(2,1)} %bitcast.34) | data formatting | bytes 26214400
  296.4 0.0 reduce-scatter.4.cloned.1.call-update
  296.5 0.0 all-gather.8.cloned.1.call-start
  296.5 79.2 %reduce-scatter.4.cloned.1.call-done = bf16[160,2560]{1,0:T(8,128)(2,1)} async-done(((bf16[2560,2560]{1,0:T(8,128)(2,1)}), bf16[160,2560]{1,0:T(8,128)(2,1)}) %reduce-scatter.4.cloned.1.call-update) | async-done | bytes 819216 | tf_op jit(solution)/shard_map/reduce_scatter | solution.py:47
  375.7 0.0 all-gather.8.cloned.1.call-update
  375.7 0.2 all-gather.6.cloned.1.call-start
  376.0 35.2 %all-gather.8.cloned.1.call-done = bf16[320,2560]{1,0:T(8,128)(2,1)} async-done(((bf16[160,2560]{1,0:T(8,128)(2,1)}), bf16[320,2560]{1,0:T(8,128)(2,1)}) %all-gather.8.cloned.1.call-update) | async-done | bytes 1638416 | tf_op jit(solution)/shard_map/all_gather | solution.py:20
  411.2 0.0 all-gather.6.cloned.1.call-update
  411.2 68.7 %all-gather.6.cloned.1.call-done = bf16[8,160,1,2560]{3,1,2,0:T(8,128)(2,1)} async-done(((bf16[2,160,1,2560]{3,1,2,0:T(8,128)(2,1)}), bf16[8,160,1,2560]{3,1,2,0:T(8,128)(2,1)}) %all-gather.6.cloned.1.call-update) | async-done | bytes 6553616 | tf_op jit(solution)/shard_map/all_gather | solution.py:20
  479.9 10.6 %copy.12 = bf16[2,4,160,1,2560]{4,1,0,2,3:T(4,128)(2,1)} copy(bf16[2,4,160,1,2560]{4,2,0,1,3:T(8,128)(2,1)} %bitcast.35) | data formatting | bytes 13107200 | tf_op jit(solution)/shard_map/transpose | solution.py:24
  490.5 11.4 %reshape.21 = bf16[8,160,1,2560]{3,0,1,2:T(8,128)(2,1)} reshape(bf16[2,4,160,1,2560]{4,1,0,2,3:T(4,128)(2,1)} %copy.12) | data formatting | bytes 13107200 | tf_op jit(solution)/shard_map/reshape | solution.py:24
  502.0 0.0 copy-done.2
  502.0 7.4 %fusion.3 = f32[2,160,2560]{2,0,1:T(2,128)S(1)} fusion(bf16[8,160,1,2560]{3,0,1,2:T(8,128)(2,1)} %reshape.21, f32[2,8]{1,0:T(2,128)S(1)} %copy-done.2), kind=kOutput, calls=%fused_computation.4 | convolution fusion | flops 78643200 | bytes 9830464 | tf_op jit(solution)/shard_map/tm,rmc->trc/dot_general | solution.py:56
  509.3 2.3 copy.13
  (3 shorter events, 0.0 us)
Async XLA Ops:
  6.5 255.5 %copy-start = (bf16[1,256,4096]{2,1,0:T(8,128)(2,1)S(1)}, bf16[1,256,4096]{2,1,0:T(8,128)(2,1)}, u32[]{:S(2)}) copy-start(bf16[1,256,4096]{2,1,0:T(8,128)(2,1)} %param.4) | copy-start | bytes 6291460
  6.5 229.0 %all-gather.10.cloned.1.call-start = ((), (), s32[]{:S(2)}) async-start(), calls=%async_computation.3 | async-start | bytes 25362432 | tf_op jit(solution)/shard_map/all_gather | solution.py:36
  7.3 254.8 %copy-start.3 = (bf16[2560,256]{1,0:T(8,128)(2,1)S(1)}, bf16[2560,256]{1,0:T(8,128)(2,1)}, u32[]{:S(2)}) copy-start(bf16[2560,256]{1,0:T(8,128)(2,1)} %param.5) | copy-start | bytes 3932164
  7.3 368.4 %reduce-scatter.4.cloned.1.call-start = ((), (), s32[]{:S(2)}) async-start(), calls=%async_computation.4 | async-start | bytes 13926400 | tf_op jit(solution)/shard_map/reduce_scatter | solution.py:47
  296.5 114.7 %all-gather.8.cloned.1.call-start = ((), (), s32[]{:S(2)}) async-start(), calls=%async_computation.2 | async-start | bytes 2457600 | tf_op jit(solution)/shard_map/all_gather | solution.py:20
  375.7 104.2 %all-gather.6.cloned.1.call-start = ((), (), s32[]{:S(2)}) async-start(), calls=%async_computation.1 | async-start | bytes 8192000 | tf_op jit(solution)/shard_map/all_gather | solution.py:20
  490.5 11.4 %copy-start.2 = (f32[2,8]{1,0:T(2,128)S(1)}, f32[2,8]{1,0:T(2,128)}, u32[]{:S(2)}) copy-start(f32[2,8]{1,0:T(2,128)} %param.7) | copy-start | bytes 196
  490.5 21.1 %copy-start.1 = (bf16[1,256,4096]{2,1,0:T(8,128)(2,1)S(1)}, bf16[1,256,4096]{2,1,0:T(8,128)(2,1)}, u32[]{:S(2)}) copy-start(bf16[1,256,4096]{2,1,0:T(8,128)(2,1)} %param.4) | copy-start | bytes 6291460
Sparse Core Ops, SparseCore 0:
  9.1 226.4 all-gather.9
  296.6 79.0 reduce-scatter.3
  377.4 33.7 all-gather.7
  412.7 67.1 all-gather.5
where the time goes:
time: 520 us; the launch traced here: 518 us
  waiting for transfers between devices  412 us (79%)
  local copies, waits for them, and re-layouts  68.5 us (13%)
  matrix products  24.1 us (5%)
  between operations  13.1 us (3%)
    all_gather x1, waiting for transfers between devices, on_device(): lax.all_gather(expand_in, LAYER_WIDTH, axis=0, tiled=True)  228 us
    all_gather x2, waiting for transfers between devices, stacked_from(): parts = lax.all_gather(parts, axes[k], axis=0, tiled=True)  104 us
    reduce_scatter x1, waiting for transfers between devices, on_device(): lax.psum_scatter(partial_value.astype(jnp.float32).reshape(own_rows * lax...  79.2 us
    unnamed x10, local copies, waits for them, and re-layouts  44.1 us
    dot_general x1, matrix products, on_device(): jnp.einsum('ri,kic->rkc', expand_out, projected, preferred_element_type=j...  16.7 us
    reshape x1, local copies, waits for them, and re-layouts, stacked_from(): parts.transpose(*turned, *range(len(order), parts.ndim))  11.4 us
    transpose x1, local copies, waits for them, and re-layouts, stacked_from(): parts.transpose(*turned, *range(len(order), parts.ndim))  10.6 us
  transfers between devices with their start and end apart: 4, of which 4 were waited for; matrix products, arithmetic and copies ran while one was open for 0% of the time, Pallas kernels for 0%

commit v1 on v0

v1 whole, which is shorter than its diff:
```python
import jax
import jax.numpy as jnp
from jax import lax
from jax.experimental import pallas as pl
from jax.experimental.pallas import tpu as pltpu
from jax.sharding import Mesh
from jax.sharding import PartitionSpec as P

AXES = ("hi", "x", "lo", "z", "c")
NS = 5
NT = (((1,), (1,)), ((), ()))
F32 = jnp.float32
BF16 = jnp.bfloat16


def mod(value, n):
    return lax.rem(value, n)


def kernel(
    src, eo_in, e_in, depth, out,
    zbuf, eb, sb, eo, pt, pbuf, lbuf, rbuf, rel, zf, ra, bs, xq, xg, tb, fin, d_oth, cf,
    send, recv, loc,
):
    hi, x, lo, z, c = (lax.axis_index(a) for a in AXES)
    y = hi * 2 + lo

    def dev(dx=0, dy=0, dz=0, core=None):
        ny = mod(y + dy + 4, 4)
        return (
            lax.div(ny, 2), mod(x + dx + 4, 4), mod(ny, 2), mod(z + dz + 4, 4),
            c if core is None else core,
        )

    a_side = (hi, x, 1 - lo, z)
    b_side = (1 - hi, x, 1 - lo, z)
    partner = dev(core=1 - c)

    count = [0]
    started = []

    def remote(src_ref, dst_ref, device, slot=None):
        i = count[0]
        count[0] += 1
        return pltpu.make_async_remote_copy(
            src_ref=src_ref, dst_ref=dst_ref, send_sem=send.at[i],
            recv_sem=recv.at[i] if slot is None else recv.at[slot],
            device_id=device, device_id_type=pl.DeviceIdType.MESH,
        )

    def go(copy):
        copy.start()
        started.append(copy)
        return copy

    barrier = pltpu.get_barrier_semaphore()
    peers = [dev(dx=d) for d in (1, -1, 2)] + [dev(dy=2)] + [dev(dz=d) for d in (1, -1, 2)] + [partner]
    peers += [a_side + (k,) for k in (0, 1)] + [b_side + (k,) for k in (0, 1)]
    for peer in peers:
        pl.semaphore_signal(barrier, inc=1, device_id=peer, device_id_type=pl.DeviceIdType.MESH)
    pl.semaphore_wait(barrier, len(peers))

    zloc = pltpu.make_async_copy(e_in, zbuf.at[z], loc.at[0])
    zloc.start()
    zsend = [go(remote(e_in, zbuf.at[z], dev(dz=d))) for d in (1, -1, 2)]

    local = []
    local.append(pltpu.make_async_copy(src.at[0], sb.at[pl.ds(0, 256)], loc.at[1]))
    shared = [remote(src.at[0], sb.at[pl.ds(256, 256)], partner)]
    for p in range(2):
        for d in range(4):
            row = pl.multiple_of(p * 1280 + mod(z + d, 4) * 320, 320)
            piece = eo_in.at[pl.ds(row, 320)]
            local.append(pltpu.make_async_copy(piece, eo.at[p * 4 + d, :, pl.ds(0, 256)], loc.at[2 + p * 4 + d]))
            shared.append(remote(piece, eo.at[p * 4 + d, :, pl.ds(256, 256)], partner))
    for copy in local:
        copy.start()
    for copy in shared:
        go(copy)
    dsend = go(remote(depth, d_oth, b_side + (c,)))

    zloc.wait()
    for copy in zsend:
        copy.wait_recv()

    def at16(s):
        place = (x * 4 + y) if s % 2 == 0 else (y * 4 + x)
        return pl.multiple_of(place * 16, 16)

    for s in range(4):
        eb[s, pl.ds(at16(s), 16), :] = zbuf[s, 0:16, :]
    eb[4, pl.ds(at16(4), 16), :] = jnp.concatenate(
        [zbuf[k, 16:20, :].astype(F32) for k in range(4)], axis=0
    ).astype(BF16)

    st = [dict() for _ in range(NS)]

    def small(s):
        rows = eb.at[s, pl.ds(at16(s), 16)]
        mine = zbuf.at[s, pl.ds(0, 16)] if s < 4 else rows
        st[s]["small"] = [
            go(remote(mine, rows, dev(dy=d) if s % 2 == 0 else dev(dx=d))) for d in (1, -1, 2)
        ]

    def along(s, d):
        return dev(dx=d) if s % 2 == 0 else dev(dy=d)

    def line(s, d, first=0, rows=64):
        main = x if s % 2 == 0 else y
        return eb.at[s, pl.ds(pl.multiple_of(mod(main + d + 4, 4) * 64 + first, 16), rows)]

    def large(s):
        for copy in st[s]["small"]:
            copy.wait_recv()
        st[s]["large"] = [go(remote(line(s, 0), line(s, 0), along(s, d))) for d in (1, -1)]

    def forward(s):
        right, left = st[s]["large"]
        right.wait_recv()
        one = go(remote(line(s, -1, 0, 32), line(s, -1, 0, 32), along(s, 1)))
        left.wait_recv()
        two = go(remote(line(s, 1, 32, 32), line(s, 1, 32, 32), along(s, -1)))
        st[s]["forward"] = [one, two]

    def compute(s):
        for copy in st[s]["forward"]:
            copy.wait_recv()
        pt[...] = lax.dot_general(eb[s], sb[...], NT, preferred_element_type=F32).astype(BF16)

        def rows_of(k, _):
            pbuf[s, k] = lax.dot_general(eo[k], pt[...], NT, preferred_element_type=F32).astype(BF16)
            return 0

        lax.fori_loop(0, 8, rows_of, 0)
        right, left = dev(dz=1), dev(dz=-1)
        st[s]["r1"] = go(remote(pbuf.at[s, 2], lbuf.at[s, 0], right))
        st[s]["l1"] = go(remote(pbuf.at[s, 6], rbuf.at[s, 0], left))
        st[s]["r2"] = go(remote(pbuf.at[s, 5], lbuf.at[s, 1], right))
        st[s]["l2"] = go(remote(pbuf.at[s, 3], rbuf.at[s, 1], left))

    def relay(s):
        st[s]["r1"].wait_recv()
        rel[s, 0] = (pbuf[s, 1].astype(F32) + lbuf[s, 0].astype(F32)).astype(BF16)
        st[s]["r3"] = go(remote(rel.at[s, 0], lbuf.at[s, 2], dev(dz=1)))
        st[s]["l1"].wait_recv()
        rel[s, 1] = (pbuf[s, 7].astype(F32) + rbuf[s, 0].astype(F32)).astype(BF16)
        st[s]["l3"] = go(remote(rel.at[s, 1], rbuf.at[s, 2], dev(dz=-1)))

    def part(s, p, k):
        return zf.at[s, p, pl.ds(pl.multiple_of(k * 160, 160), 160)]

    def settle(s):
        for name in ("l2", "r2", "r3", "l3"):
            st[s][name].wait_recv()
        zf[s, 0] = (pbuf[s, 0].astype(F32) + lbuf[s, 2].astype(F32) + rbuf[s, 1].astype(F32)).astype(BF16)
        zf[s, 1] = (pbuf[s, 4].astype(F32) + rbuf[s, 2].astype(F32) + lbuf[s, 1].astype(F32)).astype(BF16)
        st[s]["a1"] = go(remote(part(s, 1 - lo, 1 - hi), ra.at[s, 1], a_side + (c,)))
        st[s]["a0"] = go(remote(part(s, lo, hi), ra.at[s, 0], a_side + (c,)))

    def pair(s):
        st[s]["a1"].wait_recv()
        bs[s] = (part(s, lo, 1 - hi)[...].astype(F32) + ra[s, 1].astype(F32)).astype(BF16)
        st[s]["b"] = go(remote(bs.at[s], xq.at[s, 1], b_side + (c,)))
        st[s]["a0"].wait_recv()
        xq[s, 0] = (part(s, 1 - lo, hi)[...].astype(F32) + ra[s, 0].astype(F32)).astype(BF16)
        st[s]["x0"] = [go(remote(xq.at[s, 0], xg.at[s, k, 0], dev(dx=d))) for k, d in ((0, 1), (1, -1))]

    def second(s):
        st[s]["b"].wait_recv()
        st[s]["x1"] = [go(remote(xq.at[s, 1], xg.at[s, k, 1], dev(dx=d))) for k, d in ((0, 1), (1, -1))]

    def onward(s):
        st[s]["x0"][0].wait_recv()
        st[s]["f0"] = go(remote(xg.at[s, 0, 0], xg.at[s, 2, 0], dev(dx=1)))
        st[s]["x1"][1].wait_recv()
        st[s]["f1"] = go(remote(xg.at[s, 1, 1], xg.at[s, 2, 1], dev(dx=-1)))

    def coefficients():
        dsend.wait_recv()
        column = lax.broadcasted_iota(jnp.int32, (2, 8), 1)
        for h in range(2):
            values = (depth if h == 0 else d_oth)[...]
            for p in range(2):
                half = hi if p == 0 else 1 - hi
                for k, d in enumerate((0, -1, 1, 2)):
                    which = half * 4 + mod(x + d + 4, 4)
                    one = jnp.sum(jnp.where(column == which, values, 0.0), axis=1, keepdims=True)
                    for t in range(2):
                        row = (h * 2 + t) * 8 + p * 4 + k
                        cf[row : row + 1, :] = jnp.broadcast_to(one[t : t + 1, :], (1, 256))

    back = 150

    def mix(s):
        st[s]["x0"][1].wait_recv()
        st[s]["x1"][0].wait_recv()
        st[s]["f0"].wait_recv()
        st[s]["f1"].wait_recv()

        def block(i, _):
            rows = pl.ds(pl.multiple_of(i * 16, 16), 16)
            total = [None] * 4
            for p in range(2):
                for k in range(4):
                    value = (xq[s, p, rows, :] if k == 0 else xg[s, k - 1, p, rows, :]).astype(F32)
                    for g in range(4):
                        row = g * 8 + p * 4 + k
                        term = cf[row : row + 1, :] * value
                        total[g] = term if total[g] is None else total[g] + term
            for g in range(4):
                tb[s, g, rows, :] = total[g].astype(BF16)
            return 0

        lax.fori_loop(0, 10, block, 0)
        place = fin.at[c, s]
        st[s]["t"] = [
            go(remote(tb.at[s, pl.ds(0, 2)], place, a_side + (hi,), slot=back + c * NS + s)),
            go(remote(tb.at[s, pl.ds(2, 2)], place, b_side + (hi,), slot=back + c * NS + s)),
        ]

    def finish(s):
        for k in range(2):
            pltpu.make_async_remote_copy(
                src_ref=tb.at[s, pl.ds(0, 2)], dst_ref=fin.at[k, s], send_sem=send.at[0],
                recv_sem=recv.at[back + k * NS + s],
                device_id=a_side + (c,), device_id_type=pl.DeviceIdType.MESH,
            ).wait_recv()
        r = lax.broadcasted_iota(jnp.int32, (256, 1), 0)
        i = lax.rem(r, 16)
        if s % 2 == 0:
            xx, yy = lax.div(r, 64), lax.rem(lax.div(r, 16), 4)
        else:
            yy, xx = lax.div(r, 64), lax.rem(lax.div(r, 16), 4)
        group = (lax.div(yy, 2) * 4 + xx) * 2 + lax.rem(yy, 2)
        if s < 4:
            target = group * 160 + s * 40 + i
        else:
            target = group * 160 + lax.div(i, 4) * 40 + 16 + lax.rem(i, 4)
        lane = lax.broadcasted_iota(jnp.int32, (256, 256), 1)

        def columns(n, _):
            first = pl.multiple_of(n * 256, 256)
            for t in range(2):
                total = None
                for k in range(2):
                    pick = jnp.where(lane + first == target + k * 20, 1.0, 0.0).astype(BF16)
                    term = jnp.dot(fin[k, s, t], pick, preferred_element_type=F32)
                    total = term if total is None else total + term
                where = (t, slice(None), pl.ds(first, 256))
                out[where] = total if s == 0 else out[where] + total
            return 0

        lax.fori_loop(0, 10, columns, 0)

    small(0); small(1)
    large(0); large(1); small(2); small(3)
    coefficients()
    for copy in local:
        copy.wait()
    forward(0); forward(1); large(2); large(3); small(4)
    for copy in shared:
        copy.wait_recv()
    compute(0); compute(1)
    relay(0); relay(1); forward(2); forward(3); large(4)
    settle(0); settle(1); compute(2); compute(3)
    pair(0); pair(1); relay(2); relay(3); second(0); second(1); forward(4)
    onward(0); onward(1); settle(2); settle(3); compute(4); mix(0); mix(1)
    pair(2); pair(3); relay(4); second(2); second(3); finish(0); finish(1)
    onward(2); onward(3); settle(4); pair(4); mix(2); mix(3); second(4); finish(2); onward(4)
    finish(3); mix(4); finish(4)

    for copy in started:
        copy.wait_send()


def on_device(source, expand_out, expand_in, depth):
    any_space = pl.BlockSpec(memory_space=pl.ANY)
    vmem = pl.BlockSpec(memory_space=pltpu.VMEM)
    return pl.pallas_call(
        kernel,
        out_shape=jax.ShapeDtypeStruct((2, 160, 2560), F32),
        in_specs=[any_space, any_space, any_space, vmem],
        out_specs=vmem,
        scratch_shapes=[
            pltpu.VMEM((4, 20, 4096), BF16),
            pltpu.VMEM((NS, 256, 4096), BF16),
            pltpu.VMEM((512, 4096), BF16),
            pltpu.VMEM((8, 320, 512), BF16),
            pltpu.VMEM((256, 512), BF16),
            pltpu.VMEM((NS, 8, 320, 256), BF16),
            pltpu.VMEM((NS, 3, 320, 256), BF16),
            pltpu.VMEM((NS, 3, 320, 256), BF16),
            pltpu.VMEM((NS, 2, 320, 256), BF16),
            pltpu.VMEM((NS, 2, 320, 256), BF16),
            pltpu.VMEM((NS, 2, 160, 256), BF16),
            pltpu.VMEM((NS, 160, 256), BF16),
            pltpu.VMEM((NS, 2, 160, 256), BF16),
            pltpu.VMEM((NS, 3, 2, 160, 256), BF16),
            pltpu.VMEM((NS, 4, 160, 256), BF16),
            pltpu.VMEM((2, NS, 2, 160, 256), BF16),
            pltpu.VMEM((2, 8), F32),
            pltpu.VMEM((32, 256), F32),
            pltpu.SemaphoreType.DMA((160,)),
            pltpu.SemaphoreType.DMA((160,)),
            pltpu.SemaphoreType.DMA((10,)),
        ],
        compiler_params=pltpu.CompilerParams(
            collective_id=0, has_side_effects=True, vmem_limit_bytes=66 * 1024 * 1024 - 2 * 1024 * 1024 - 70 * 1024,
        ),
    )(source, expand_out, expand_in, depth)


def solution(mesh):
    finer = Mesh(mesh.devices.reshape(2, 4, 2, 4, 2), AXES)
    layer, width = ("hi", "x"), ("lo", "z", "c")
    return jax.shard_map(
        on_device,
        mesh=finer,
        in_specs=(P(layer, width, None), P(None, width), P(layer + width, None), P(layer, None)),
        out_specs=P(layer, width, None),
        check_vma=False,
    )
```

time: 520 us -> 153 us (0.29)
  waiting for transfers between devices: 412 us -> 0 us
  Pallas kernels: 0 us -> 149 us
  local copies, waits for them, and re-layouts: 68.5 us -> 3.85 us
  matrix products: 24.1 us -> 0 us
  between operations: 13.1 us -> 0.01 us
    all_gather x3 -> x0, waiting for transfers between devices: 332 us -> none  [the longest x1 228 us: on_device(): lax.all_gather(expand_in, LAYER_WIDTH, axis=0, tiled=True)]
    pallas_call x0 -> x1, Pallas kernels: none -> 149 us  [on_device(): pl.pallas_call(kernel, out_shape=jax.ShapeDtypeStruct((2, 160, 2560), F32...]
    reduce_scatter x1 -> x0, waiting for transfers between devices: 79.2 us -> none  [on_device(): lax.psum_scatter(partial_value.astype(jnp.float32).reshape(own_rows * lax...]
    unnamed x10 -> x1, local copies, waits for them, and re-layouts: 44.1 us -> 3.85 us
    dot_general x2 -> x0, matrix products: 24.1 us -> none  [the longest x1 16.7 us: on_device(): jnp.einsum('ri,kic->rkc', expand_out, projected, preferred_element_type=j...]
    reshape x1 -> x0, local copies, waits for them, and re-layouts: 11.4 us -> none  [stacked_from(): parts.transpose(*turned, *range(len(order), parts.ndim))]
    transpose x1 -> x0, local copies, waits for them, and re-layouts: 10.6 us -> none  [stacked_from(): parts.transpose(*turned, *range(len(order), parts.ndim))]
  transfers between devices with their start and end apart: 4 -> 0, of which waited for: 4 -> 0; matrix products, arithmetic and copies ran while one was open for 0% -> 0% of each run, Pallas kernels for 0% -> 0%
where the time goes in v1:
time: 153 us
  Pallas kernels  149 us (97%)
  local copies, waits for them, and re-layouts  3.85 us (3%)
    pallas_call x1, Pallas kernels, on_device(): pl.pallas_call(kernel, out_shape=jax.ShapeDtypeStruct((2, 160, 2560), F32...  149 us
    unnamed x1, local copies, waits for them, and re-layouts  3.85 us

profile of v1, /device:TPU:1, one launch (start us, length us, event | category | flops | bytes accessed | tf_op | source)
XLA Modules:
  0.0 152.7 jit_solution(15090338740324856976)
XLA Ops:
  0.0 148.8 %shard_map.46 = f32[2,160,2560]{2,1,0:T(8,128)} custom-call(bf16[1,256,4096]{2,1,0:T(8,128)(2,1)} %src.1, bf16[2560,256]{1,0:T(8,128)(2,1)} %eo_in.1, bf16[20,4096]{1,0:T(8,128)(2,1)} %e_in.1, f32[2,8]{1,0:T(2,128)} %depth.1), custom_call_target="tpu_custom_call" | custom-call | tf_op jit(solution)/shard_map/pallas_call | solution.py:279
  148.9 3.9 %copy.6 = f32[2,160,2560]{2,1,0:T(8,128)} copy(f32[2,160,2560]{2,1,0:T(8,128)} %shard_map.46) | data formatting | bytes 6553600
